TPU v7x, 32 devices: a whole 2x2x4 slice. The times are simulated.
32 devices in a mesh: node: 4 (over z), slab: 8 (over y, x, core).
Axes of the slice: x: 2, y: 2, z: 4, core: 2. Of those that a mesh axis runs over, the one named last changes fastest.
Arguments:
- initial: float32 [32, 256, 256], P('slab'), may hold values from -20 to 20
- sections: float32 [4, 32, 256, 256], P('node', 'slab'), may hold values from -21 to 21
Outputs:
- new_sections: float32 [4, 32, 256, 256], P('node', 'slab')
- residual_max: float32 [3], replicated
All inputs are finite; a program needn't handle non-finite values.
Results may differ from a plain program's by a relative error of at most 0.0003.
Values sent between devices are 32-bit elements; how exact they have to be, the bound alone decides.
A program may use at most 64 MiB of HBM per device.

v0:
```python
import math

import jax
import jax.numpy as jnp
from jax import lax
from jax.sharding import PartitionSpec as P

SWEEPS = 3


diffusion_step = 4.0
highest = lax.Precision.HIGHEST


def with_halo(block, sides, width):
    for axis, dim in sides:
        count = lax.axis_size(axis)
        forward = [(i, i + 1) for i in range(count - 1)]
        forward.append((count - 1, 0))
        backward = [(target, source) for source, target in forward]
        low = lax.ppermute(
            lax.slice_in_dim(block, block.shape[dim] - width, None, axis=dim), axis, forward
        )
        high = lax.ppermute(lax.slice_in_dim(block, 0, width, axis=dim), axis, backward)
        block = jnp.concatenate([low, block, high], axis=dim)
    return block


def radau_value(order, point):
    prev_value = 1.0
    prev_slope = 0.0
    this_value = point
    this_slope = 1.0
    for degree in range(1, order):
        next_value = ((2 * degree + 1) * point * this_value - degree * prev_value) / (degree + 1)
        next_slope = (
            (2 * degree + 1) * (this_value + point * this_slope) - degree * prev_slope
        ) / (degree + 1)
        prev_value, prev_slope = (this_value, this_slope)
        this_value, this_slope = (next_value, next_slope)
    return (this_value - prev_value, this_slope - prev_slope)


def radau_tables(node_total):
    points = []
    for node_index in range(node_total):
        estimate = math.cos(2.0 * math.pi * node_index / (2 * node_total - 1))
        if node_index > 0:
            for repeat in range(60):
                poly_value, poly_slope = radau_value(node_total, estimate)
                estimate = estimate - poly_value / poly_slope
        points.append((estimate + 1.0) / 2.0)
    points = sorted(points)
    quadrature = []
    for row_index in range(node_total):
        entries = []
        for column_index in range(node_total):
            coeffs = [1.0]
            for other_index in range(node_total):
                if other_index != column_index:
                    divisor = points[column_index] - points[other_index]
                    shifted = [0.0] + coeffs
                    widened = coeffs + [0.0]
                    coeffs = [
                        (shifted[place] - points[other_index] * widened[place]) / divisor
                        for place in range(len(shifted))
                    ]
            integral = 0.0
            for place in range(len(coeffs)):
                integral = integral + coeffs[place] * points[row_index] ** (place + 1) / (place + 1)
            entries.append(integral)
        quadrature.append(entries)
    return (points, quadrature)


def cas_table(length):
    indices = lax.iota(jnp.int32, length)
    products = indices[:, None] * indices[None, :] % length
    phases = products.astype(jnp.float32) * (2.0 * math.pi / length)
    return jnp.cos(phases) + jnp.sin(phases)


def eigen_line(length):
    indices = lax.iota(jnp.int32, length).astype(jnp.float32)
    return 2.0 * jnp.cos(indices * (2.0 * math.pi / length)) - 2.0


def laplacian(grid_values):
    padded = with_halo(grid_values, (("slab", 0),), 1)
    center = padded[1:-1]
    beside = padded[2:] + padded[:-2]
    beside = beside + jnp.roll(center, 1, 1) + jnp.roll(center, -1, 1)
    beside = beside + jnp.roll(center, 1, 2) + jnp.roll(center, -1, 2)
    return beside - 6.0 * center


def on_device(initial, sections):
    node_count = lax.axis_size("node")
    slab_count = lax.axis_size("slab")
    slab_cells, cells_y, cells_z = initial.shape
    total_x = slab_cells * slab_count
    scale_back = 1.0 / float(total_x * cells_y * cells_z)
    nodes_list, quad_list = radau_tables(node_count)
    nodes_at = jnp.asarray(nodes_list, jnp.float32)
    quadrature = jnp.asarray(quad_list, jnp.float32)
    my_node = lax.axis_index("node")
    node_ids = lax.iota(jnp.int32, node_count)
    my_point = jnp.sum(jnp.where(node_ids == my_node, nodes_at, 0.0))
    cas_x = cas_table(total_x)
    cas_y = cas_table(cells_y)
    cas_z = cas_table(cells_z)
    column_rows = cells_y // slab_count
    eigen_y = lax.dynamic_slice_in_dim(
        eigen_line(cells_y), lax.axis_index("slab") * column_rows, column_rows, 0
    )
    spectrum = (
        eigen_line(total_x)[:, None, None]
        + eigen_y[None, :, None]
        + eigen_line(cells_z)[None, None, :]
    )
    maxima = []
    current = sections[0]
    for sweep_index in range(SWEEPS):
        slopes = laplacian(current)
        blended = jnp.einsum(
            "mj,jcyz->mcyz",
            quadrature,
            lax.all_to_all(slopes[None], "node", split_axis=3, concat_axis=0, tiled=True),
            precision=highest,
        )
        combined = lax.all_to_all(blended, "node", split_axis=0, concat_axis=3, tiled=True)[0]
        residual = initial + diffusion_step * combined - current
        maxima.append(jnp.max(jnp.abs(residual)))
        diagonal = my_point / (sweep_index + 1.0)
        right_side = initial + diffusion_step * (combined - diagonal * slopes)
        spectral = jnp.einsum("cyz,zw->cyw", right_side, cas_z, precision=highest)
        spectral = jnp.einsum("cyw,yv->cvw", spectral, cas_y, precision=highest)
        columns = lax.all_to_all(spectral, "slab", split_axis=1, concat_axis=0, tiled=True)
        columns = jnp.einsum("xyw,xa->ayw", columns, cas_x, precision=highest)
        columns = columns / (1.0 - diffusion_step * diagonal * spectrum)
        columns = jnp.einsum("xyw,xa->ayw", columns, cas_x, precision=highest)
        returned = lax.all_to_all(columns, "slab", split_axis=0, concat_axis=1, tiled=True)
        returned = jnp.einsum("cyw,yv->cvw", returned, cas_y, precision=highest)
        returned = jnp.einsum("cyz,zw->cyw", returned, cas_z, precision=highest)
        current = returned * scale_back
    result = lax.pmax(jnp.stack(maxima), ("node", "slab"))
    return (current[None], result)


def solution(mesh):
    placed = (P("slab", None, None), P("node", "slab", None, None))
    return jax.shard_map(
        on_device,
        mesh=mesh,
        in_specs=placed,
        out_specs=(P("node", "slab", None, None), P()),
        check_vma=False,
    )
```

profile of v0, /device:TPU:0, one launch (start us, length us, event | category | flops | bytes accessed | tf_op | source)
XLA Modules:
  0.0 432.4 jit_solution(7158053486910289120)
XLA Ops:
  6.0 5.0 %collective-permute-done = f32[1,256,256]{2,1,0:T(8,128)S(1)} collective-permute-done((f32[1,256,256]{2,1,0:T(8,128)S(1)}, f32[1,256,256]{2,1,0:T(8,128)S(1)}, u32[]{:S(2)}, u32[]{:S(2)}) %collective-permute-start) | collective-permute-done | bytes 262176 | tf_op jit(solution)/shard_map/ppermute | solution.py:24
  14.9 28.3 %all_to_all.207 = f32[1,4,256,256]{2,1,0,3:T(4,128)S(1)} all-to-all(f32[1,4,256,256]{2,1,0,3:T(4,128)} %copy.73), channel_id=1, replica_groups=mesh['node'=4,'slab'=8] {'node'}, dimensions={3} | all-to-all | bytes 2097152 | tf_op jit(solution)/shard_map/all_to_all | solution.py:128
  46.6 3.5 all-to-all-start.1
  51.4 22.7 %all-to-all-done.1 = f32[4,4,256,64]{2,3,1,0:T(8,128)S(1)} async-done(((f32[4,4,256,64]{2,3,1,0:T(8,128)}), f32[4,4,256,64]{2,3,1,0:T(8,128)S(1)}, u32[]{:S(2)}, u32[]{:S(2)}) %all-to-all-start.1) | async-done | bytes 1048608 | tf_op jit(solution)/shard_map/all_to_all | solution.py:131
  77.9 4.0 fusion.44
  85.6 7.1 %all-to-all-start.2 = ((f32[4,256,256]{2,0,1:T(4,128)}), f32[4,256,256]{2,0,1:T(4,128)S(1)}, u32[]{:S(2)}, u32[]{:S(2)}) async-start(f32[4,256,256]{2,0,1:T(4,128)} %copy.80), calls=%async_computation.2 | async-start | bytes 2097152 | tf_op jit(solution)/shard_map/all_to_all | solution.py:138
  93.6 14.4 %all-to-all-done.2 = f32[4,256,256]{2,0,1:T(4,128)S(1)} async-done(((f32[4,256,256]{2,0,1:T(4,128)}), f32[4,256,256]{2,0,1:T(4,128)S(1)}, u32[]{:S(2)}, u32[]{:S(2)}) %all-to-all-start.2) | async-done | bytes 1048608 | tf_op jit(solution)/shard_map/all_to_all | solution.py:138
  111.7 17.8 %all_to_all.208 = f32[32,32,256]{2,1,0:T(8,128)S(1)} all-to-all(f32[32,32,256]{2,1,0:T(8,128)S(1)} %copy.84), channel_id=1, replica_groups=mesh['node'=4,'slab'=8] {'slab'}, dimensions={0} | all-to-all | bytes 2097152 | tf_op jit(solution)/shard_map/all_to_all | solution.py:142
  135.1 5.7 %collective-permute-done.2 = f32[1,256,256]{2,1,0:T(8,128)S(1)} collective-permute-done((f32[1,256,256]{2,1,0:T(8,128)S(1)}, f32[1,256,256]{2,1,0:T(8,128)S(1)}, u32[]{:S(2)}, u32[]{:S(2)}) %collective-permute-start.2) | collective-permute-done | bytes 262176 | tf_op jit(solution)/shard_map/ppermute | solution.py:24
  144.4 28.8 %all_to_all.209 = f32[1,4,256,256]{2,1,0,3:T(4,128)S(1)} all-to-all(f32[1,4,256,256]{2,1,0,3:T(4,128)} %copy.87), channel_id=1, replica_groups=mesh['node'=4,'slab'=8] {'node'}, dimensions={3} | all-to-all | bytes 2097152 | tf_op jit(solution)/shard_map/all_to_all | solution.py:128
  176.7 4.3 all-to-all-start.5
  181.6 24.2 %all-to-all-done.5 = f32[4,4,256,64]{2,3,1,0:T(8,128)} async-done(((f32[4,4,256,64]{2,3,1,0:T(8,128)}), f32[4,4,256,64]{2,3,1,0:T(8,128)}, u32[]{:S(2)}, u32[]{:S(2)}) %all-to-all-start.5) | async-done | bytes 1048608 | tf_op jit(solution)/shard_map/all_to_all | solution.py:131
  217.7 5.6 %all-to-all-start.6 = ((f32[4,256,256]{2,0,1:T(4,128)}), f32[4,256,256]{2,0,1:T(4,128)S(1)}, u32[]{:S(2)}, u32[]{:S(2)}) async-start(f32[4,256,256]{2,0,1:T(4,128)} %copy.94), calls=%async_computation.6 | async-start | bytes 2097152 | tf_op jit(solution)/shard_map/all_to_all | solution.py:138
  223.9 14.7 %all-to-all-done.6 = f32[4,256,256]{2,0,1:T(4,128)S(1)} async-done(((f32[4,256,256]{2,0,1:T(4,128)}), f32[4,256,256]{2,0,1:T(4,128)S(1)}, u32[]{:S(2)}, u32[]{:S(2)}) %all-to-all-start.6) | async-done | bytes 1048608 | tf_op jit(solution)/shard_map/all_to_all | solution.py:138
  242.3 17.8 %all_to_all.210 = f32[32,32,256]{2,1,0:T(8,128)S(1)} all-to-all(f32[32,32,256]{2,1,0:T(8,128)S(1)} %copy.98), channel_id=1, replica_groups=mesh['node'=4,'slab'=8] {'slab'}, dimensions={0} | all-to-all | bytes 2097152 | tf_op jit(solution)/shard_map/all_to_all | solution.py:142
  265.7 5.7 %collective-permute-done.4 = f32[1,256,256]{2,1,0:T(8,128)S(1)} collective-permute-done((f32[1,256,256]{2,1,0:T(8,128)S(1)}, f32[1,256,256]{2,1,0:T(8,128)S(1)}, u32[]{:S(2)}, u32[]{:S(2)}) %collective-permute-start.4) | collective-permute-done | bytes 262176 | tf_op jit(solution)/shard_map/ppermute | solution.py:24
  274.9 28.6 %all_to_all.211 = f32[1,4,256,256]{2,1,0,3:T(4,128)S(1)} all-to-all(f32[1,4,256,256]{2,1,0,3:T(4,128)} %copy.101), channel_id=1, replica_groups=mesh['node'=4,'slab'=8] {'node'}, dimensions={3} | all-to-all | bytes 2097152 | tf_op jit(solution)/shard_map/all_to_all | solution.py:128
  307.1 4.3 all-to-all-start.9
  312.0 24.2 %all-to-all-done.9 = f32[4,4,256,64]{2,3,1,0:T(8,128)} async-done(((f32[4,4,256,64]{2,3,1,0:T(8,128)}), f32[4,4,256,64]{2,3,1,0:T(8,128)}, u32[]{:S(2)}, u32[]{:S(2)}) %all-to-all-start.9) | async-done | bytes 1048608 | tf_op jit(solution)/shard_map/all_to_all | solution.py:131
  348.0 5.6 %all-to-all-start.10 = ((f32[4,256,256]{2,0,1:T(4,128)}), f32[4,256,256]{2,0,1:T(4,128)S(1)}, u32[]{:S(2)}, u32[]{:S(2)}) async-start(f32[4,256,256]{2,0,1:T(4,128)} %copy.108), calls=%async_computation.10 | async-start | bytes 2097152 | tf_op jit(solution)/shard_map/all_to_all | solution.py:138
  354.3 14.7 %all-to-all-done.10 = f32[4,256,256]{2,0,1:T(4,128)S(1)} async-done(((f32[4,256,256]{2,0,1:T(4,128)}), f32[4,256,256]{2,0,1:T(4,128)S(1)}, u32[]{:S(2)}, u32[]{:S(2)}) %all-to-all-start.10) | async-done | bytes 1048608 | tf_op jit(solution)/shard_map/all_to_all | solution.py:138
  373.7 4.4 %all-to-all-start.11 = ((f32[32,32,256]{2,1,0:T(8,128)}), f32[32,32,256]{2,1,0:T(8,128)}, u32[]{:S(2)}, u32[]{:S(2)}) async-start(f32[32,32,256]{2,1,0:T(8,128)} %copy.112), calls=%async_computation.11 | async-start | bytes 2097152 | tf_op jit(solution)/shard_map/all_to_all | solution.py:142
  383.1 41.6 %pmax.7 = f32[3]{0:T(128)} all-reduce(f32[3]{0:T(128)S(1)} %pad_maximum_fusion.6), channel_id=1, replica_groups=mesh['node'=4,'slab'=8] {'node','slab'}, use_global_device_ids=true, to_apply=%region_4.5 | all-reduce | flops 3 | bytes 24 | tf_op jit(solution)/shard_map/pmax | solution.py:146
  428.1 3.8 fusion
  (95 shorter events, 91.0 us)
Async XLA Ops:
  0.6 4.6 %copy-start = (f32[1,4,256,256]{3,2,1,0:T(8,128)S(1)}, f32[1,4,256,256]{3,2,1,0:T(8,128)}, u32[]{:S(2)}) copy-start(f32[1,4,256,256]{3,2,1,0:T(8,128)} %param.5) | copy-start | bytes 3145732
  1.8 9.2 %collective-permute-start = (f32[1,256,256]{2,1,0:T(8,128)S(1)}, f32[1,256,256]{2,1,0:T(8,128)S(1)}, u32[]{:S(2)}, u32[]{:S(2)}) collective-permute-start(f32[1,256,256]{2,1,0:T(8,128)S(1)} %get-tuple-element.33), channel_id=1, source_target_pairs={{1,0},{2,1},{3,2},{4,3},{5,4},{6,5},{7,6},{0,7},{9,8},{10,9},{11,1... | collective-permute-start | bytes 786440 | tf_op jit(solution)/shard_map/ppermute | solution.py:24
  5.2 7.7 %collective-permute-start.1 = (f32[1,256,256]{2,1,0:T(8,128)S(1)}, f32[1,256,256]{2,1,0:T(8,128)S(1)}, u32[]{:S(2)}, u32[]{:S(2)}) collective-permute-start(f32[1,256,256]{2,1,0:T(8,128)S(1)} %get-tuple-element.34), channel_id=1, source_target_pairs={{0,1},{1,2},{2,3},{3,4},{4,5},{5,6},{6,7},{7,0},{8,9},{9,10},{10,1... | collective-permute-start | bytes 786440 | tf_op jit(solution)/shard_map/ppermute | solution.py:21
  14.9 28.3 %copy-start.5 = (f32[4,4,1,1]{1,0,3,2:T(4,128)S(1)}, f32[4,4,1,1]{1,0,3,2:T(4,128)}, u32[]{:S(2)}) copy-start(f32[4,4,1,1]{1,0,3,2:T(4,128)} %constant.87) | copy-start | bytes 196
  46.6 27.5 %all-to-all-start.1 = ((f32[4,4,256,64]{2,3,1,0:T(8,128)}), f32[4,4,256,64]{2,3,1,0:T(8,128)S(1)}, u32[]{:S(2)}, u32[]{:S(2)}) async-start(f32[4,4,256,64]{2,3,1,0:T(8,128)} %copy.76), calls=%async_computation.1 | async-start | bytes 2097152 | tf_op jit(solution)/shard_map/all_to_all | solution.py:131
  50.2 0.7 copy-start.6
  75.2 2.6 copy-start.1
  85.6 22.4 %all-to-all-start.2 = ((f32[4,256,256]{2,0,1:T(4,128)}), f32[4,256,256]{2,0,1:T(4,128)S(1)}, u32[]{:S(2)}, u32[]{:S(2)}) async-start(f32[4,256,256]{2,0,1:T(4,128)} %copy.80), calls=%async_computation.2 | async-start | bytes 2097152 | tf_op jit(solution)/shard_map/all_to_all | solution.py:138
  133.7 8.7 %copy-start.2 = (f32[4,256,256]{2,1,0:T(8,128)}, f32[4,256,256]{2,1,0:T(8,128)S(1)}, u32[]{:S(2)}) copy-start(f32[4,256,256]{2,1,0:T(8,128)S(1)} %get-tuple-element.36) | copy-start | bytes 3145732
  134.4 6.4 %collective-permute-start.2 = (f32[1,256,256]{2,1,0:T(8,128)S(1)}, f32[1,256,256]{2,1,0:T(8,128)S(1)}, u32[]{:S(2)}, u32[]{:S(2)}) collective-permute-start(f32[1,256,256]{2,1,0:T(8,128)S(1)} %get-tuple-element.23), channel_id=1, source_target_pairs={{1,0},{2,1},{3,2},{4,3},{5,4},{6,5},{7,6},{0,7},{9,8},{10,9},{11,1... | collective-permute-start | bytes 786440 | tf_op jit(solution)/shard_map/ppermute | solution.py:24
  134.4 8.0 %collective-permute-start.3 = (f32[1,256,256]{2,1,0:T(8,128)S(1)}, f32[1,256,256]{2,1,0:T(8,128)S(1)}, u32[]{:S(2)}, u32[]{:S(2)}) collective-permute-start(f32[1,256,256]{2,1,0:T(8,128)S(1)} %get-tuple-element.24), channel_id=1, source_target_pairs={{0,1},{1,2},{2,3},{3,4},{4,5},{5,6},{6,7},{7,0},{8,9},{9,10},{10,1... | collective-permute-start | bytes 786440 | tf_op jit(solution)/shard_map/ppermute | solution.py:21
  176.7 29.1 %all-to-all-start.5 = ((f32[4,4,256,64]{2,3,1,0:T(8,128)}), f32[4,4,256,64]{2,3,1,0:T(8,128)}, u32[]{:S(2)}, u32[]{:S(2)}) async-start(f32[4,4,256,64]{2,3,1,0:T(8,128)} %copy.90), calls=%async_computation.5 | async-start | bytes 2097152 | tf_op jit(solution)/shard_map/all_to_all | solution.py:131
  217.7 20.9 %all-to-all-start.6 = ((f32[4,256,256]{2,0,1:T(4,128)}), f32[4,256,256]{2,0,1:T(4,128)S(1)}, u32[]{:S(2)}, u32[]{:S(2)}) async-start(f32[4,256,256]{2,0,1:T(4,128)} %copy.94), calls=%async_computation.6 | async-start | bytes 2097152 | tf_op jit(solution)/shard_map/all_to_all | solution.py:138
  264.3 8.7 %copy-start.4 = (f32[4,256,256]{2,1,0:T(8,128)}, f32[4,256,256]{2,1,0:T(8,128)S(1)}, u32[]{:S(2)}) copy-start(f32[4,256,256]{2,1,0:T(8,128)S(1)} %get-tuple-element.38) | copy-start | bytes 3145732
  264.9 6.4 %collective-permute-start.4 = (f32[1,256,256]{2,1,0:T(8,128)S(1)}, f32[1,256,256]{2,1,0:T(8,128)S(1)}, u32[]{:S(2)}, u32[]{:S(2)}) collective-permute-start(f32[1,256,256]{2,1,0:T(8,128)S(1)} %get-tuple-element.13), channel_id=1, source_target_pairs={{1,0},{2,1},{3,2},{4,3},{5,4},{6,5},{7,6},{0,7},{9,8},{10,9},{11,1... | collective-permute-start | bytes 786440 | tf_op jit(solution)/shard_map/ppermute | solution.py:24
  265.0 8.0 %collective-permute-start.5 = (f32[1,256,256]{2,1,0:T(8,128)S(1)}, f32[1,256,256]{2,1,0:T(8,128)S(1)}, u32[]{:S(2)}, u32[]{:S(2)}) collective-permute-start(f32[1,256,256]{2,1,0:T(8,128)S(1)} %get-tuple-element.14), channel_id=1, source_target_pairs={{0,1},{1,2},{2,3},{3,4},{4,5},{5,6},{6,7},{7,0},{8,9},{9,10},{10,1... | collective-permute-start | bytes 786440 | tf_op jit(solution)/shard_map/ppermute | solution.py:21
  307.1 29.1 %all-to-all-start.9 = ((f32[4,4,256,64]{2,3,1,0:T(8,128)}), f32[4,4,256,64]{2,3,1,0:T(8,128)}, u32[]{:S(2)}, u32[]{:S(2)}) async-start(f32[4,4,256,64]{2,3,1,0:T(8,128)} %copy.104), calls=%async_computation.9 | async-start | bytes 2097152 | tf_op jit(solution)/shard_map/all_to_all | solution.py:131
  348.0 21.0 %all-to-all-start.10 = ((f32[4,256,256]{2,0,1:T(4,128)}), f32[4,256,256]{2,0,1:T(4,128)S(1)}, u32[]{:S(2)}, u32[]{:S(2)}) async-start(f32[4,256,256]{2,0,1:T(4,128)} %copy.108), calls=%async_computation.10 | async-start | bytes 2097152 | tf_op jit(solution)/shard_map/all_to_all | solution.py:138
  373.7 4.4 %copy-start.3 = (f32[4,256,256]{2,1,0:T(8,128)S(1)}, f32[4,256,256]{2,1,0:T(8,128)}, u32[]{:S(2)}) copy-start(f32[4,256,256]{2,1,0:T(8,128)} %copy-done.2) | copy-start | bytes 3145732
  373.7 51.0 %all-to-all-start.11 = ((f32[32,32,256]{2,1,0:T(8,128)}), f32[32,32,256]{2,1,0:T(8,128)}, u32[]{:S(2)}, u32[]{:S(2)}) async-start(f32[32,32,256]{2,1,0:T(8,128)} %copy.112), calls=%async_computation.11 | async-start | bytes 2097152 | tf_op jit(solution)/shard_map/all_to_all | solution.py:142
where the time goes:
time: 441 us; the launch traced here: 432 us
  blocking collectives  163 us (37%)
  waiting for transfers between devices  137 us (31%)
  matrix products  46.3 us (10%)
  starting transfers between devices  39.2 us (9%)
  local copies, waits for them, and re-layouts  35.1 us (8%)
  other arithmetic  7.66 us (2%)
  between operations  4.76 us (1%)
    all_to_all x3, blocking collectives, on_device(): lax.all_to_all(slopes[None], 'node', split_axis=3, concat_axis=0, tiled=T...  85.7 us
    all_to_all x3, waiting for transfers between devices, on_device(): lax.all_to_all(blended, 'node', split_axis=0, concat_axis=3, tiled=True)[0]  71.1 us
    all_to_all x3, waiting for transfers between devices, on_device(): lax.all_to_all(spectral, 'slab', split_axis=1, concat_axis=0, tiled=True)  43.8 us
    pmax x1, blocking collectives, on_device(): result = lax.pmax(jnp.stack(maxima), ('node', 'slab'))  41.6 us
    all_to_all x2, blocking collectives, on_device(): lax.all_to_all(columns, 'slab', split_axis=0, concat_axis=1, tiled=True)  35.5 us
    all_to_all x3, starting transfers between devices, on_device(): lax.all_to_all(spectral, 'slab', split_axis=1, concat_axis=0, tiled=True)  18.3 us
    ppermute x3, waiting for transfers between devices, with_halo(): lax.ppermute(lax.slice_in_dim(block, 0, width, axis=dim), axis, backward)  16.4 us
    all_to_all x3, starting transfers between devices, on_device(): lax.all_to_all(blended, 'node', split_axis=0, concat_axis=3, tiled=True)[0]  12 us
  transfers between devices with their start and end apart: 13, of which 12 were waited for; matrix products, arithmetic and copies ran while one was open for 2% of the time, Pallas kernels for 0%

commit v1 on v0

v1 whole, which is shorter than its diff:
```python
import math

import jax
import jax.numpy as jnp
from jax import lax
from jax.sharding import PartitionSpec as P

SWEEPS = 3


diffusion_step = 4.0
high = lax.Precision.HIGH


def radau_value(order, point):
    prev_value = 1.0
    prev_slope = 0.0
    this_value = point
    this_slope = 1.0
    for degree in range(1, order):
        next_value = ((2 * degree + 1) * point * this_value - degree * prev_value) / (degree + 1)
        next_slope = (
            (2 * degree + 1) * (this_value + point * this_slope) - degree * prev_slope
        ) / (degree + 1)
        prev_value, prev_slope = (this_value, this_slope)
        this_value, this_slope = (next_value, next_slope)
    return (this_value - prev_value, this_slope - prev_slope)


def radau_tables(node_total):
    points = []
    for node_index in range(node_total):
        estimate = math.cos(2.0 * math.pi * node_index / (2 * node_total - 1))
        if node_index > 0:
            for repeat in range(60):
                poly_value, poly_slope = radau_value(node_total, estimate)
                estimate = estimate - poly_value / poly_slope
        points.append((estimate + 1.0) / 2.0)
    points = sorted(points)
    quadrature = []
    for row_index in range(node_total):
        entries = []
        for column_index in range(node_total):
            coeffs = [1.0]
            for other_index in range(node_total):
                if other_index != column_index:
                    divisor = points[column_index] - points[other_index]
                    shifted = [0.0] + coeffs
                    widened = coeffs + [0.0]
                    coeffs = [
                        (shifted[place] - points[other_index] * widened[place]) / divisor
                        for place in range(len(shifted))
                    ]
            integral = 0.0
            for place in range(len(coeffs)):
                integral = integral + coeffs[place] * points[row_index] ** (place + 1) / (place + 1)
            entries.append(integral)
        quadrature.append(entries)
    return (points, quadrature)


def cas_table(length):
    indices = lax.iota(jnp.int32, length)
    products = indices[:, None] * indices[None, :] % length
    phases = products.astype(jnp.float32) * (2.0 * math.pi / length)
    return jnp.cos(phases) + jnp.sin(phases)


def eigen_line(length):
    indices = lax.iota(jnp.int32, length).astype(jnp.float32)
    return 2.0 * jnp.cos(indices * (2.0 * math.pi / length)) - 2.0


def on_device(initial, sections):
    node_count = lax.axis_size("node")
    slab_count = lax.axis_size("slab")
    both = ("node", "slab")
    total_count = node_count * slab_count
    slab_cells, cells_y, cells_z = initial.shape
    total_x = slab_cells * slab_count
    share = max(slab_cells // node_count, 1)
    repeats = max(node_count // slab_cells, 1)
    rows = cells_y // total_count
    scale_back = 1.0 / float(total_x * cells_y * cells_z)
    nodes_list, quad_list = radau_tables(node_count)
    my_node = lax.axis_index("node")
    my_place = my_node * slab_count + lax.axis_index("slab")
    cas_x = cas_table(total_x)
    cas_y = cas_table(cells_y)
    cas_z = cas_table(cells_z)
    eigen_y = lax.dynamic_slice_in_dim(eigen_line(cells_y), my_place * rows, rows, 0)
    spectrum = (
        eigen_line(total_x)[:, None, None]
        + eigen_y[None, :, None]
        + eigen_line(cells_z)[None, None, :]
    )
    mine = lax.dynamic_slice_in_dim(initial, my_node // repeats * share, share, 0)
    planes = jnp.concatenate([sections[0], mine], axis=0)
    planes = jnp.einsum("cyz,yv->cvz", planes, cas_y, precision=high)
    pencils = lax.all_to_all(planes, both, split_axis=1, concat_axis=0, tiled=True)
    pencils = jnp.einsum("cyz,zw->cyw", pencils, cas_z, precision=high)
    pencils = pencils.reshape(node_count, slab_count, slab_cells + share, rows, cells_z)
    iterate = jnp.einsum(
        "nsiyw,sia->nayw",
        pencils[:, :, :slab_cells],
        cas_x.reshape(slab_count, slab_cells, total_x),
        precision=high,
    )
    start = jnp.einsum(
        "nsiyw,snia->ayw",
        pencils[::repeats, :, slab_cells:],
        cas_x.reshape(slab_count, node_count // repeats, share, total_x),
        precision=high,
    )
    values = [iterate[m] for m in range(node_count)]
    stretched = diffusion_step * spectrum
    residuals = []
    for m in range(node_count):
        mixed = sum(quad_list[m][j] * values[j] for j in range(node_count))
        residuals.append(start + stretched * mixed - values[m])
    fields = [jnp.stack(residuals)]
    for sweep_index in range(SWEEPS):
        change = []
        for m in range(node_count):
            weight = nodes_list[m] / (sweep_index + 1.0)
            change.append(residuals[m] / (1.0 - weight * stretched))
        values = [values[m] + change[m] for m in range(node_count)]
        if sweep_index + 1 < SWEEPS:
            slopes = [stretched * change[m] for m in range(node_count)]
            residuals = [
                residuals[m]
                - change[m]
                + sum(quad_list[m][j] * slopes[j] for j in range(node_count))
                for m in range(node_count)
            ]
            fields.append(jnp.stack(residuals))
    fields.append(jnp.stack(values))
    fields = jnp.stack(fields)
    back_x = cas_x.reshape(total_x, slab_count, slab_cells) * scale_back
    outward = jnp.einsum("fmayw,asi->msfiyw", fields, back_x, precision=high)
    outward = jnp.einsum("msfiyw,wz->msfiyz", outward, cas_z, precision=high)
    outward = outward.reshape(-1, rows, cells_z)
    arrived = lax.all_to_all(outward, both, split_axis=0, concat_axis=1, tiled=True)
    arrived = jnp.einsum("cyz,yv->cvz", arrived, cas_y, precision=high)
    arrived = arrived.reshape(SWEEPS + 1, slab_cells, cells_y, cells_z)
    largest = jnp.max(jnp.abs(arrived[:SWEEPS]), axis=(1, 2, 3))
    spread = jnp.broadcast_to(largest[None], (total_count, SWEEPS))
    result = jnp.max(
        lax.all_to_all(spread, both, split_axis=0, concat_axis=0, tiled=True), axis=0
    )
    return (arrived[SWEEPS:], result)


def solution(mesh):
    placed = (P("slab", None, None), P("node", "slab", None, None))
    return jax.shard_map(
        on_device,
        mesh=mesh,
        in_specs=placed,
        out_specs=(P("node", "slab", None, None), P()),
        check_vma=False,
    )
```

time: 441 us -> 192 us (0.44); the launches traced: 432 us -> 191 us
  waiting for transfers between devices: 137 us -> 53.2 us
  blocking collectives: 163 us -> 97.5 us
  matrix products: 46.3 us -> 17.3 us
  starting transfers between devices: 39.2 us -> 11.2 us
  local copies, waits for them, and re-layouts: 35.1 us -> 9.09 us
  other arithmetic: 7.66 us -> 2.31 us
    all_to_all x7 -> x2, waiting for transfers between devices: 115 us -> 53.2 us  [the longest x1 48.3 us: on_device(): lax.all_to_all(planes, both, split_axis=1, concat_axis=0, tiled=True)]
    pmax x1 -> x0, blocking collectives: 41.6 us -> none  [on_device(): result = lax.pmax(jnp.stack(maxima), ('node', 'slab'))]
    dot_general x21 -> x7, matrix products: 46.3 us -> 17.3 us  [the longest x1 4.16 us: on_device(): outward = jnp.einsum('msfiyw,wz->msfiyz', outward, cas_z, precision=high)]
    all_to_all x5 -> x1, blocking collectives: 121 us -> 97.5 us  [on_device(): lax.all_to_all(outward, both, split_axis=0, concat_axis=1, tiled=True)]
    all_to_all x7 -> x2, starting transfers between devices: 34.7 us -> 11.2 us  [the longest x1 7.51 us: on_device(): lax.all_to_all(planes, both, split_axis=1, concat_axis=0, tiled=True)]
    ppermute x6 -> x0, waiting for transfers between devices: 21.6 us -> none  [the longest x3 16.4 us: with_halo(): lax.ppermute(lax.slice_in_dim(block, 0, width, axis=dim), axis, backward)]
    squeeze x3 -> x0, local copies, waits for them, and re-layouts: 7.72 us -> none  [on_device(): lax.all_to_all(blended, 'node', split_axis=0, concat_axis=3, tiled=True)[0]]
    all_to_all x12 -> x1, local copies, waits for them, and re-layouts: 8.1 us -> 0.55 us  [on_device(): lax.all_to_all(planes, both, split_axis=1, concat_axis=0, tiled=True)]
  transfers between devices with their start and end apart: 13 -> 2, of which waited for: 12 -> 2; matrix products, arithmetic and copies ran while one was open for 2% -> 1% of each run, Pallas kernels for 0% -> 0%
where the time goes in v1:
time: 192 us; the launch traced here: 191 us
  blocking collectives  97.5 us (51%)
  waiting for transfers between devices  53.2 us (28%)
  matrix products  17.3 us (9%)
  starting transfers between devices  11.2 us (6%)
  local copies, waits for them, and re-layouts  9.09 us (5%)
  other arithmetic  2.31 us (1%)
    all_to_all x1, blocking collectives, on_device(): lax.all_to_all(outward, both, split_axis=0, concat_axis=1, tiled=True)  97.5 us
    all_to_all x1, waiting for transfers between devices, on_device(): lax.all_to_all(planes, both, split_axis=1, concat_axis=0, tiled=True)  48.3 us
    all_to_all x1, starting transfers between devices, on_device(): lax.all_to_all(planes, both, split_axis=1, concat_axis=0, tiled=True)  7.51 us
    all_to_all x1, waiting for transfers between devices, on_device(): lax.all_to_all(spread, both, split_axis=0, concat_axis=0, tiled=True)  4.89 us
    dot_general x1, matrix products, on_device(): outward = jnp.einsum('msfiyw,wz->msfiyz', outward, cas_z, precision=high)  4.16 us
  transfers between devices with their start and end apart: 2, of which 2 were waited for; matrix products, arithmetic and copies ran while one was open for 1% of the time, Pallas kernels for 0%

profile of v1, /device:TPU:0, one launch (start us, length us, event | category | flops | bytes accessed | tf_op | source)
XLA Modules:
  0.0 191.3 jit_solution(9316244434102739991)
XLA Ops:
  0.6 1.2 copy-done
  1.9 3.0 %convolution_bitcast_fusion = f32[5,256,256]{2,1,0:T(8,128)S(1)} fusion(f32[1,256,256]{2,1,0:T(8,128)S(1)} %constant_dynamic-slice_fusion, f32[4,256,256]{2,1,0:T(8,128)} %bitcast.162), kind=kOutput, calls=%fused_computation.42 | convolution fusion | flops 504627200 | bytes 2621440 | tf_op jit(solution)/shard_map/cyz,yv->cvz/dot_general | solution.py:99
  4.9 2.2 %copy.36 = f32[5,256,256]{2,0,1:T(8,128)} copy(f32[5,256,256]{2,1,0:T(8,128)S(1)} %convolution_bitcast_fusion) | data formatting | bytes 2621440 | tf_op jit(solution)/shard_map/cyz,yv->cvz/transpose | solution.py:99
  7.0 7.5 %all-to-all-start = ((f32[5,256,256]{2,0,1:T(8,128)}), f32[5,256,256]{2,0,1:T(8,128)S(1)}, u32[]{:S(2)}, u32[]{:S(2)}) async-start(f32[5,256,256]{2,0,1:T(8,128)} %copy.36), calls=%async_computation | async-start | bytes 4194304 | tf_op jit(solution)/shard_map/all_to_all | solution.py:100
  14.8 48.3 %all-to-all-done = f32[5,256,256]{2,0,1:T(8,128)S(1)} async-done(((f32[5,256,256]{2,0,1:T(8,128)}), f32[5,256,256]{2,0,1:T(8,128)S(1)}, u32[]{:S(2)}, u32[]{:S(2)}) %all-to-all-start) | async-done | bytes 1310752 | tf_op jit(solution)/shard_map/all_to_all | solution.py:100
  63.1 0.6 copy.37
  63.6 1.7 fusion.77
  65.4 0.1 slice.38
  65.5 1.3 convolution_bitcast_fusion.1
  66.8 1.6 fusion.63
  68.4 0.8 fusion.67
  69.2 0.2 maximum_bitcast_fusion.6
  69.4 0.1 maximum_bitcast_fusion.4
  69.6 2.2 %fusion.16 = f32[4,8,4,4,8,256]{5,1,4,0,2,3:T(8,128)S(1)} fusion(f32[1,4,32,8,256]{4,2,3,1,0:T(8,128)S(1)} %get-tuple-element.25, f32[1,4,32,8,256]{4,2,3,1,0:T(8,128)S(1)} %get-tuple-element.24, f32[1,4,32,8,256]{4,2,3,1,0:T(8,128)S(1)} %get-tuple-element.23, f32[1,4,32,8,256]{4,2,3,1,0:T(8,128)S(1)} %get-tuple-element.22, s32[8,4]{0,1:T(4,128)S(1)} %multiply_add_fusion), kind=kOutput, calls=%fused_computation.16 | convolution fusion | flops 204488704 | bytes 8388736 | tf_op jit(solution)/shard_map/fmayw,asi->msfiyw/dot_general | solution.py:140
  71.7 4.2 %fusion.10 = f32[4,8,4,4,8,256]{5,4,3,2,1,0:T(8,128)S(1)} fusion(f32[4,8,4,4,8,256]{5,1,4,0,2,3:T(8,128)S(1)} %fusion.16), kind=kOutput, calls=%fused_computation.11 | convolution fusion | flops 1611595776 | bytes 8388608 | tf_op jit(solution)/shard_map/msfiyw,wz->msfiyz/dot_general | solution.py:141
  75.9 97.5 %all_to_all.39 = f32[512,8,256]{2,1,0:T(8,128)S(1)} all-to-all(f32[512,8,256]{2,1,0:T(8,128)S(1)} %bitcast.158), channel_id=1, replica_groups=mesh['node'=4,'slab'=8] {'node','slab'}, dimensions={0} | all-to-all | bytes 8388608 | tf_op jit(solution)/shard_map/all_to_all | solution.py:143
  173.4 3.4 %fusion.13 = f32[16,256,256]{2,1,0:T(8,128)S(1)} fusion(f32[32,16,8,256]{3,2,1,0:T(8,128)S(1)} %bitcast.159), kind=kOutput, calls=%fused_computation.15 | convolution fusion | flops 1611595776 | bytes 8388608 | tf_op jit(solution)/shard_map/cyz,yv->cvz/dot_general | solution.py:144
  176.8 1.9 %copy-done.1 = f32[16,256,256]{2,1,0:T(8,128)} copy-done((f32[16,256,256]{2,1,0:T(8,128)}, f32[16,256,256]{2,1,0:T(8,128)S(1)}, u32[]{:S(2)}) %copy-start.1) | copy-done | bytes 4194328
  178.7 0.3 fusion.12
  179.3 0.6 broadcast_in_dim.2
  179.9 3.7 %all-to-all-start.2 = ((f32[32,1,3]{2,1,0:T(1,128)}), f32[32,1,3]{2,1,0:T(1,128)S(1)}, u32[]{:S(2)}, u32[]{:S(2)}) async-start(f32[32,1,3]{2,1,0:T(1,128)} %broadcast_in_dim.2), calls=%async_computation.2 | async-start | bytes 32768 | tf_op jit(solution)/shard_map/all_to_all | solution.py:149
  183.6 2.3 %slice_bitcast_fusion = f32[1,4,256,256]{3,2,1,0:T(8,128)} fusion(f32[16,256,256]{2,1,0:T(8,128)} %copy-done.1), kind=kLoop, calls=%fused_computation.48 | loop fusion | bytes 2097152 | tf_op jit(solution)/shard_map/slice | solution.py:151
  185.9 4.9 %all-to-all-done.2 = f32[32,1,3]{2,1,0:T(1,128)S(1)} async-done(((f32[32,1,3]{2,1,0:T(1,128)}), f32[32,1,3]{2,1,0:T(1,128)S(1)}, u32[]{:S(2)}, u32[]{:S(2)}) %all-to-all-start.2) | async-done | bytes 416 | tf_op jit(solution)/shard_map/all_to_all | solution.py:149
  190.8 0.6 reduce_max.28
  (11 shorter events, 0.5 us)
Async XLA Ops:
  0.6 1.2 copy-start
  7.0 56.1 %all-to-all-start = ((f32[5,256,256]{2,0,1:T(8,128)}), f32[5,256,256]{2,0,1:T(8,128)S(1)}, u32[]{:S(2)}, u32[]{:S(2)}) async-start(f32[5,256,256]{2,0,1:T(8,128)} %copy.36), calls=%async_computation | async-start | bytes 4194304 | tf_op jit(solution)/shard_map/all_to_all | solution.py:100
  176.8 1.9 %copy-start.1 = (f32[16,256,256]{2,1,0:T(8,128)}, f32[16,256,256]{2,1,0:T(8,128)S(1)}, u32[]{:S(2)}) copy-start(f32[16,256,256]{2,1,0:T(8,128)S(1)} %fusion.13) | copy-start | bytes 12582916
  179.9 10.8 %all-to-all-start.2 = ((f32[32,1,3]{2,1,0:T(1,128)}), f32[32,1,3]{2,1,0:T(1,128)S(1)}, u32[]{:S(2)}, u32[]{:S(2)}) async-start(f32[32,1,3]{2,1,0:T(1,128)} %broadcast_in_dim.2), calls=%async_computation.2 | async-start | bytes 32768 | tf_op jit(solution)/shard_map/all_to_all | solution.py:149

commit v2 on v0

v2 whole, which is shorter than its diff:
```python
import functools
import math

import jax
import jax.numpy as jnp
from jax import lax
from jax.experimental import pallas as pl
from jax.experimental.pallas import tpu as pltpu
from jax.sharding import PartitionSpec as P

SWEEPS = 3


diffusion_step = 4.0
MESH = pl.DeviceIdType.MESH


def radau_value(order, point):
    prev_value = 1.0
    prev_slope = 0.0
    this_value = point
    this_slope = 1.0
    for degree in range(1, order):
        next_value = ((2 * degree + 1) * point * this_value - degree * prev_value) / (degree + 1)
        next_slope = (
            (2 * degree + 1) * (this_value + point * this_slope) - degree * prev_slope
        ) / (degree + 1)
        prev_value, prev_slope = (this_value, this_slope)
        this_value, this_slope = (next_value, next_slope)
    return (this_value - prev_value, this_slope - prev_slope)


def radau_tables(node_total):
    points = []
    for node_index in range(node_total):
        estimate = math.cos(2.0 * math.pi * node_index / (2 * node_total - 1))
        if node_index > 0:
            for repeat in range(60):
                poly_value, poly_slope = radau_value(node_total, estimate)
                estimate = estimate - poly_value / poly_slope
        points.append((estimate + 1.0) / 2.0)
    points = sorted(points)
    quadrature = []
    for row_index in range(node_total):
        entries = []
        for column_index in range(node_total):
            coeffs = [1.0]
            for other_index in range(node_total):
                if other_index != column_index:
                    divisor = points[column_index] - points[other_index]
                    shifted = [0.0] + coeffs
                    widened = coeffs + [0.0]
                    coeffs = [
                        (shifted[place] - points[other_index] * widened[place]) / divisor
                        for place in range(len(shifted))
                    ]
            integral = 0.0
            for place in range(len(coeffs)):
                integral = integral + coeffs[place] * points[row_index] ** (place + 1) / (place + 1)
            entries.append(integral)
        quadrature.append(entries)
    return (points, quadrature)


def cas_table(length):
    indices = lax.iota(jnp.int32, length)
    products = indices[:, None] * indices[None, :] % length
    phases = products.astype(jnp.float32) * (2.0 * math.pi / length)
    return jnp.cos(phases) + jnp.sin(phases)


def eigen_line(length):
    indices = lax.iota(jnp.int32, length).astype(jnp.float32)
    return 2.0 * jnp.cos(indices * (2.0 * math.pi / length)) - 2.0


def split_terms(value):
    upper = value.astype(jnp.bfloat16)
    lower = (value - upper.astype(jnp.float32)).astype(jnp.bfloat16)
    return upper, lower


def table_terms(table):
    upper = lax.reduce_precision(table, 8, 7)
    return jnp.stack([upper.astype(jnp.bfloat16), (table - upper).astype(jnp.bfloat16)])


def product(left, right):
    def one(a, b):
        return jnp.dot(a, b, preferred_element_type=jnp.float32)

    return one(left[0], right[0]) + (one(left[0], right[1]) + one(left[1], right[0]))


def loop(count, step, carry, group=4):
    group = group if count % group == 0 else 1

    def body(index, state):
        for offset in range(group):
            state = step(index * group + offset, state)
        return state

    return lax.fori_loop(0, count // group, body, carry)


def sweeps_kernel(
    nodes, quad, u, first, lam, ymat_ref, zmat_ref, out, top,
    planes, gathered, start, resid, front, outward, arrived, rho, gain, close, peak, peers, lines,
    send_u, recv_u, send_i, recv_i, send_z, recv_z, send_r, recv_r, send_m, recv_m, local,
):
    node_count, slab_count = len(nodes), lax.axis_size("slab")
    me, here = lax.axis_index("node"), lax.axis_index("slab")
    cells, size_y, size_z = u.shape
    chunks, total_x, rows = gathered.shape[0], gathered.shape[2], gathered.shape[3]
    band = chunks * rows
    scale = 1.0 / float(size_y * size_z)

    def other_slab(step):
        return lax.rem(here + step, slab_count)

    def other_node(step):
        return lax.rem(me + step, node_count)

    def to(src, dst, send, recv, node, slab):
        return pltpu.make_async_remote_copy(
            src_ref=src, dst_ref=dst, send_sem=send, recv_sem=recv,
            device_id=(node, slab), device_id_type=MESH,
        )

    barrier = pltpu.get_barrier_semaphore()
    for step in range(1, slab_count):
        pl.semaphore_signal(barrier, inc=1, device_id=(me, other_slab(step)), device_id_type=MESH)
    for step in range(1, node_count):
        pl.semaphore_signal(barrier, inc=1, device_id=(other_node(step), here), device_id_type=MESH)

    def transform(value):
        part = product(split_terms(value), (zmat_ref[0], zmat_ref[1]))
        return product((ymat_ref[0], ymat_ref[1]), split_terms(part))

    def source(field, chunk, slab):
        return planes.at[field, :, pl.ds(slab * band + chunk * rows, rows), :]

    def target(field, chunk, slab):
        span = pl.ds(slab * cells, cells)
        return gathered.at[chunk, me, span] if field == 0 else start.at[chunk, span]

    def send_field(field, send, recv):
        for chunk in range(chunks):
            pltpu.make_async_copy(
                source(field, chunk, here), target(field, chunk, here), local.at[field, chunk]
            ).start()
            for step in range(1, slab_count):
                slab = other_slab(step)
                to(
                    source(field, chunk, slab), target(field, chunk, here),
                    send.at[chunk, step], recv.at[chunk, step], me, slab,
                ).start()

    def take_field(field, chunk, send, recv):
        pltpu.make_async_copy(
            source(field, chunk, here), target(field, chunk, here), local.at[field, chunk]
        ).wait()
        for step in range(1, slab_count):
            slab = lax.rem(here + slab_count - step, slab_count)
            to(
                source(field, chunk, slab), target(field, chunk, slab),
                send.at[chunk, step], recv.at[chunk, step], me, slab,
            ).wait()

    def enter(index, state):
        planes[0, index] = transform(u[index])
        return state

    def enter_first(index, state):
        planes[1, index] = transform(first[index])
        return state

    lax.fori_loop(0, cells, enter, 0)
    pl.semaphore_wait(barrier, slab_count - 1 + node_count - 1)
    send_field(0, send_u, recv_u)
    lax.fori_loop(0, cells, enter_first, 0)
    send_field(1, send_i, recv_i)

    def piece(chunk, origin, direction):
        target_node = me + 1 if direction == 0 else me - 1
        slot = gathered.at[chunk, origin]
        return to(
            slot, slot, send_z.at[chunk, origin, direction], recv_z.at[chunk, origin],
            target_node, here,
        )

    has_right, has_left = me < node_count - 1, me > 0

    for chunk in range(chunks):
        take_field(0, chunk, send_u, recv_u)

        @pl.when(has_right)
        def _():
            piece(chunk, me, 0).start()

        @pl.when(has_left)
        def _():
            piece(chunk, me, 1).start()

    def relay(chunk):
        for away in range(1, node_count):

            @pl.when(me - away >= 0)
            def _():
                piece(chunk, me - away, 0).wait_recv()

                @pl.when(has_right)
                def _():
                    piece(chunk, me - away, 0).start()

            @pl.when(me + away < node_count)
            def _():
                piece(chunk, me + away, 1).wait_recv()

                @pl.when(has_left)
                def _():
                    piece(chunk, me + away, 1).start()

    def mix(table, values):
        mixed = []
        for line in table:
            total = line[0] * values[0]
            for weight, value in zip(line[1:], values[1:]):
                total = total + weight * value
            mixed.append(total)
        return mixed

    def solve(chunk):
        eigen = lam[pl.ds(chunk * rows, rows), :]

        def blend(x, state):
            values = [gathered[chunk, j, x] for j in range(node_count)]
            for m, value in enumerate(mix(quad, values)):
                front[x, m] = value
            return state

        def begin(x, state):
            below = lax.rem(x + total_x - 1, total_x)
            above = lax.rem(x + 1, total_x)
            for m in range(node_count):
                slope = front[below, m] + front[above, m] + (eigen - 2.0) * front[x, m]
                resid[x, m] = start[chunk, x] + diffusion_step * slope - gathered[chunk, m, x]
            return state

        loop(total_x, blend, 0)
        loop(total_x, begin, 0)
        for sweep in range(SWEEPS):
            last = sweep + 1 == SWEEPS
            for m in range(node_count):
                reach = diffusion_step * nodes[m] / (sweep + 1.0)
                excess = 1.0 / reach - eigen
                root = jnp.sqrt(excess * (excess + 4.0))
                ratio = 2.0 / (excess + 2.0 + root)
                rho[m] = ratio
                gain[m] = 1.0 / (reach * root)
                power, base, left = None, ratio, total_x
                while left:
                    if left % 2:
                        power = base if power is None else power * base
                    base, left = base * base, left // 2
                close[m] = 1.0 / (1.0 - power)
            pick = pl.ds(me, 1) if last else pl.ds(0, node_count)
            width = 1 if last else node_count
            ratio = rho[pick]
            factor = gain[pick]

            def gather_ends(x, state):
                up, down = state
                return (resid[x, pick] + ratio * up, resid[total_x - 1 - x, pick] + ratio * down)

            zero = jnp.zeros((width, rows, size_z), jnp.float32)
            up, down = loop(total_x, gather_ends, (zero, zero))
            closing = close[pick]

            def forward(x, state):
                state = resid[x, pick] + ratio * state
                front[x, pick] = state
                outward[chunk, sweep, x] = resid[x, me]
                return state

            def backward(index, state):
                x = total_x - 1 - index
                held = resid[x, pick]
                beyond = ratio * state
                change = factor * (front[x, pick] + beyond)
                front[x, pick] = change
                if sweep == 0:
                    outward[chunk, SWEEPS, x] = front[x, me]
                else:
                    outward[chunk, SWEEPS, x] = outward[chunk, SWEEPS, x] + front[x, me]
                if not last:
                    moved = change - held
                    table = [
                        [quad[m][j] * (sweep + 1.0) / nodes[j] - (1.0 if m == j else 0.0)
                         for j in range(node_count)]
                        for m in range(node_count)
                    ]
                    for m, value in enumerate(mix(table, [moved[j] for j in range(node_count)])):
                        resid[x, m] = value
                return held + beyond

            loop(total_x, forward, up * closing)
            loop(total_x, backward, down * closing, 2)

    def back_source(chunk, slab):
        return outward.at[chunk, :, pl.ds(slab * cells, cells)]

    def back_target(chunk, slab):
        return arrived.at[:, :, pl.ds(slab * band + chunk * rows, rows), :]

    for chunk in range(chunks):
        relay(chunk)
        take_field(1, chunk, send_i, recv_i)
        solve(chunk)
        pltpu.make_async_copy(
            back_source(chunk, here), back_target(chunk, here), local.at[2, chunk]
        ).start()
        for step in range(1, slab_count):
            slab = other_slab(step)
            to(
                back_source(chunk, slab), back_target(chunk, here),
                send_r.at[chunk, step], recv_r.at[chunk, step], me, slab,
            ).start()
    for chunk in range(chunks):
        pltpu.make_async_copy(
            back_source(chunk, here), back_target(chunk, here), local.at[2, chunk]
        ).wait()
        for step in range(1, slab_count):
            slab = lax.rem(here + slab_count - step, slab_count)
            to(
                back_source(chunk, slab), back_target(chunk, slab),
                send_r.at[chunk, step], recv_r.at[chunk, step], me, slab,
            ).wait()
        for origin in range(node_count):

            @pl.when(jnp.logical_and(has_right, origin <= me))
            def _():
                piece(chunk, origin, 0).wait_send()

            @pl.when(jnp.logical_and(has_left, origin >= me))
            def _():
                piece(chunk, origin, 1).wait_send()

    peak[...] = jnp.zeros_like(peak)
    for sweep in range(SWEEPS):

        def finish(index, state):
            value = jnp.abs(transform(arrived[sweep, index]))
            return jnp.maximum(state, jnp.max(value.reshape(-1, 8, size_z), axis=0))

        most = lax.fori_loop(0, cells, finish, jnp.zeros((8, size_z), jnp.float32))
        most = jnp.max(jnp.max(most, axis=1, keepdims=True), axis=0, keepdims=True) * scale
        peak[sweep : sweep + 1, :] = jnp.broadcast_to(most, (1, peak.shape[1]))

    def swap(count, slots, level, place):
        for step in range(1, count):
            to(peak, slots.at[step], send_m.at[level, step], recv_m.at[level, step], *place(step)).start()

    def settle(count, slots, level, place):
        for step in range(1, count):
            to(peak, slots.at[step], send_m.at[level, step], recv_m.at[level, step], *place(step)).wait()
        best = peak[...]
        for step in range(1, count):
            best = jnp.maximum(best, slots[step])
        return best

    def along_slab(step):
        return (me, other_slab(step))

    def along_node(step):
        return (other_node(step), here)

    def leave(index, state):
        out[index] = u[index] + scale * transform(arrived[SWEEPS, index])
        return state

    swap(slab_count, peers, 0, along_slab)
    lax.fori_loop(0, cells // 2, leave, 0)
    peak[...] = settle(slab_count, peers, 0, along_slab)
    swap(node_count, lines, 1, along_node)
    lax.fori_loop(cells // 2, cells, leave, 0)
    top[...] = settle(node_count, lines, 1, along_node)


def on_device(initial, sections):
    node_count = lax.axis_size("node")
    slab_count = lax.axis_size("slab")
    cells, size_y, size_z = initial.shape
    total_x = cells * slab_count
    nodes, quad = radau_tables(node_count)
    band = size_y // slab_count
    rows = 8
    chunks = band // rows
    eigen_y = lax.dynamic_slice_in_dim(
        eigen_line(size_y), lax.axis_index("slab") * band, band, 0
    )
    lam = eigen_y[:, None] + eigen_line(size_z)[None, :]
    matrix_y = table_terms(cas_table(size_y))
    matrix_z = table_terms(cas_table(size_z))
    whole = pl.BlockSpec(memory_space=pltpu.VMEM)

    def room(*shape):
        return pltpu.VMEM(shape, jnp.float32)

    dma = pltpu.SemaphoreType.DMA
    out, top = pl.pallas_call(
        functools.partial(sweeps_kernel, nodes, quad),
        out_shape=(
            jax.ShapeDtypeStruct((cells, size_y, size_z), jnp.float32),
            jax.ShapeDtypeStruct((8, 128), jnp.float32),
        ),
        in_specs=[whole] * 5,
        out_specs=(whole, whole),
        scratch_shapes=[
            room(2, cells, size_y, size_z),
            room(chunks, node_count, total_x, rows, size_z),
            room(chunks, total_x, rows, size_z),
            room(total_x, node_count, rows, size_z),
            room(total_x, node_count, rows, size_z),
            room(chunks, SWEEPS + 1, total_x, rows, size_z),
            room(SWEEPS + 1, cells, size_y, size_z),
            room(node_count, rows, size_z),
            room(node_count, rows, size_z),
            room(node_count, rows, size_z),
            room(8, 128),
            room(slab_count, 8, 128),
            room(node_count, 8, 128),
            dma((chunks, slab_count)),
            dma((chunks, slab_count)),
            dma((chunks, slab_count)),
            dma((chunks, slab_count)),
            dma((chunks, node_count, 2)),
            dma((chunks, node_count)),
            dma((chunks, slab_count)),
            dma((chunks, slab_count)),
            dma((2, max(slab_count, node_count))),
            dma((2, max(slab_count, node_count))),
            dma((3, chunks)),
        ],
        compiler_params=pltpu.CompilerParams(
            collective_id=0, has_side_effects=True, vmem_limit_bytes=60 * 1024 * 1024
        ),
    )(sections[0], initial, lam, matrix_y, matrix_z)
    return (out[None], top[:SWEEPS, 0])


def solution(mesh):
    placed = (P("slab", None, None), P("node", "slab", None, None))
    return jax.shard_map(
        on_device,
        mesh=mesh,
        in_specs=placed,
        out_specs=(P("node", "slab", None, None), P()),
        check_vma=False,
    )
```

time: 441 us -> 125 us (0.28); the launches traced: 432 us -> 124 us
  blocking collectives: 163 us -> 0 us
  waiting for transfers between devices: 137 us -> 0 us
  Pallas kernels: 0 us -> 117 us
  matrix products: 46.3 us -> 0 us
  starting transfers between devices: 39.2 us -> 0 us
  local copies, waits for them, and re-layouts: 35.1 us -> 3.66 us
  other arithmetic: 7.66 us -> 2.58 us
    all_to_all x5 -> x0, blocking collectives: 121 us -> none  [the longest x3 85.7 us: on_device(): lax.all_to_all(slopes[None], 'node', split_axis=3, concat_axis=0, tiled=T...]
    pallas_call x0 -> x1, Pallas kernels: none -> 117 us  [on_device(): pl.pallas_call(functools.partial(sweeps_kernel, nodes, quad), out_shape=(...]
    all_to_all x7 -> x0, waiting for transfers between devices: 115 us -> none  [the longest x3 71.1 us: on_device(): lax.all_to_all(blended, 'node', split_axis=0, concat_axis=3, tiled=True)[0]]
    dot_general x21 -> x0, matrix products: 46.3 us -> none  [the longest x3 10.6 us: on_device(): spectral = jnp.einsum('cyz,zw->cyw', right_side, cas_z, precision=highest)]
    pmax x1 -> x0, blocking collectives: 41.6 us -> none  [on_device(): result = lax.pmax(jnp.stack(maxima), ('node', 'slab'))]
    all_to_all x7 -> x0, starting transfers between devices: 34.7 us -> none  [the longest x3 18.3 us: on_device(): lax.all_to_all(spectral, 'slab', split_axis=1, concat_axis=0, tiled=True)]
    ppermute x6 -> x0, waiting for transfers between devices: 21.6 us -> none  [the longest x3 16.4 us: with_halo(): lax.ppermute(lax.slice_in_dim(block, 0, width, axis=dim), axis, backward)]
    all_to_all x12 -> x0, local copies, waits for them, and re-layouts: 8.1 us -> none  [the longest x3 5.65 us: on_device(): lax.all_to_all(blended, 'node', split_axis=0, concat_axis=3, tiled=True)[0]]
  transfers between devices with their start and end apart: 13 -> 0, of which waited for: 12 -> 0; matrix products, arithmetic and copies ran while one was open for 2% -> 0% of each run, Pallas kernels for 0% -> 0%
where the time goes in v2:
time: 125 us; the launch traced here: 124 us
  Pallas kernels  117 us (94%)
  local copies, waits for them, and re-layouts  3.66 us (3%)
  other arithmetic  2.58 us (2%)
    pallas_call x1, Pallas kernels, on_device(): pl.pallas_call(functools.partial(sweeps_kernel, nodes, quad), out_shape=(...  117 us
    unnamed x3, local copies, waits for them, and re-layouts  2.96 us

profile of v2, /device:TPU:0, one launch (start us, length us, event | category | flops | bytes accessed | tf_op | source)
XLA Modules:
  0.0 124.3 jit_solution(3170125992725847763)
XLA Ops:
  0.7 0.1 dynamic_slice.3
  0.8 0.7 broadcast_add_fusion.lam
  1.5 1.1 reduce-precision_convert_fusion
  2.6 0.7 pad_maximum_fusion.ymat_ref.zmat_ref
  3.3 117.4 %shard_map.41 = (f32[4,256,256]{2,1,0:T(8,128)}, f32[8,128]{1,0:T(8,128)}) custom-call(f32[4,256,256]{2,1,0:T(8,128)} %bitcast.3, f32[4,256,256]{2,1,0:T(8,128)} %first.1, f32[32,256]{1,0:T(8,128)} %broadcast_add_fusion.lam, bf16[2,256,256]{2,1,0:T(8,128)(2,1)} %pad_maximum_fusion.ymat_ref.zmat_ref, bf16[2,256,256]{2,1,0:T(8,128)(2,1)} %pad_maximum_fusion.ymat_ref.zmat_ref), custom_call_target="tpu_custom_call" | custom-call | tf_op jit(solution)/shard_map/pallas_call | solution.py:411
  120.7 0.0 copy-start
  120.7 0.7 copy-done
  121.4 0.6 slice_reduce_fusion
  122.0 2.3 %copy.5 = f32[1,4,256,256]{3,2,1,0:T(8,128)} copy(f32[1,4,256,256]{3,2,1,0:T(8,128)} %bitcast.2) | data formatting | bytes 2097152
  (1 shorter events, 0.0 us)
Async XLA Ops:
  120.7 0.7 copy-start

commit v3 on v2

--- a/solution.py
+++ b/solution.py
@@ -111,8 +111,9 @@
     node_count, slab_count = len(nodes), lax.axis_size("slab")
     me, here = lax.axis_index("node"), lax.axis_index("slab")
     cells, size_y, size_z = u.shape
-    chunks, total_x, rows = gathered.shape[0], gathered.shape[2], gathered.shape[3]
-    band = chunks * rows
+    chunks, _, total_x, rows, lanes = gathered.shape
+    parts = size_z // lanes
+    band = chunks // parts * rows
     scale = 1.0 / float(size_y * size_z)
 
     def other_slab(step):
@@ -137,8 +138,13 @@
         part = product(split_terms(value), (zmat_ref[0], zmat_ref[1]))
         return product((ymat_ref[0], ymat_ref[1]), split_terms(part))
 
+    def place_of(chunk, slab):
+        first_row = slab * band + chunk // parts * rows
+        return pl.ds(first_row, rows), pl.ds(chunk % parts * lanes, lanes)
+
     def source(field, chunk, slab):
-        return planes.at[field, :, pl.ds(slab * band + chunk * rows, rows), :]
+        span, columns = place_of(chunk, slab)
+        return planes.at[field, :, span, columns]
 
     def target(field, chunk, slab):
         span = pl.ds(slab * cells, cells)
@@ -191,7 +197,7 @@
 
     has_right, has_left = me < node_count - 1, me > 0
 
-    for chunk in range(chunks):
+    def launch(chunk):
         take_field(0, chunk, send_u, recv_u)
 
         @pl.when(has_right)
@@ -202,24 +208,27 @@
         def _():
             piece(chunk, me, 1).start()
 
-    def relay(chunk):
+    def forward_on(chunk, away):
+        @pl.when(jnp.logical_and(me - away >= 0, has_right))
+        def _():
+            piece(chunk, me - away, 0).wait_recv()
+            piece(chunk, me - away, 0).start()
+
+        @pl.when(jnp.logical_and(me + away < node_count, has_left))
+        def _():
+            piece(chunk, me + away, 1).wait_recv()
+            piece(chunk, me + away, 1).start()
+
+    def absorb(chunk):
         for away in range(1, node_count):
 
-            @pl.when(me - away >= 0)
+            @pl.when(jnp.logical_and(me - away >= 0, me == node_count - 1))
             def _():
                 piece(chunk, me - away, 0).wait_recv()
 
-                @pl.when(has_right)
-                def _():
-                    piece(chunk, me - away, 0).start()
-
-            @pl.when(me + away < node_count)
+            @pl.when(jnp.logical_and(me + away < node_count, me == 0))
             def _():
                 piece(chunk, me + away, 1).wait_recv()
-
-                @pl.when(has_left)
-                def _():
-                    piece(chunk, me + away, 1).start()
 
     def mix(table, values):
         mixed = []
@@ -231,7 +240,12 @@
         return mixed
 
     def solve(chunk):
-        eigen = lam[pl.ds(chunk * rows, rows), :]
+        eigen = lam[pl.ds(chunk // parts * rows, rows), pl.ds(chunk % parts * lanes, lanes)]
+
+        def between(stage):
+            if chunk + 1 < chunks:
+                for away in range(1 + stage, node_count, SWEEPS):
+                    forward_on(chunk + 1, away)
 
         def blend(x, state):
             values = [gathered[chunk, j, x] for j in range(node_count)]
@@ -250,6 +264,7 @@
         loop(total_x, blend, 0)
         loop(total_x, begin, 0)
         for sweep in range(SWEEPS):
+            between(sweep)
             last = sweep + 1 == SWEEPS
             for m in range(node_count):
                 reach = diffusion_step * nodes[m] / (sweep + 1.0)
@@ -273,7 +288,7 @@
                 up, down = state
                 return (resid[x, pick] + ratio * up, resid[total_x - 1 - x, pick] + ratio * down)
 
-            zero = jnp.zeros((width, rows, size_z), jnp.float32)
+            zero = jnp.zeros((width, rows, lanes), jnp.float32)
             up, down = loop(total_x, gather_ends, (zero, zero))
             closing = close[pick]
 
@@ -311,10 +326,17 @@
         return outward.at[chunk, :, pl.ds(slab * cells, cells)]
 
     def back_target(chunk, slab):
-        return arrived.at[:, :, pl.ds(slab * band + chunk * rows, rows), :]
-
+        span, columns = place_of(chunk, slab)
+        return arrived.at[:, :, span, columns]
+
+    for chunk in range(min(2, chunks)):
+        launch(chunk)
+    for away in range(1, node_count):
+        forward_on(0, away)
     for chunk in range(chunks):
-        relay(chunk)
+        if chunk + 2 < chunks:
+            launch(chunk + 2)
+        absorb(chunk)
         take_field(1, chunk, send_i, recv_i)
         solve(chunk)
         pltpu.make_async_copy(
@@ -395,7 +417,8 @@
     nodes, quad = radau_tables(node_count)
     band = size_y // slab_count
     rows = 8
-    chunks = band // rows
+    lanes = 128
+    chunks = band // rows * (size_z // lanes)
     eigen_y = lax.dynamic_slice_in_dim(
         eigen_line(size_y), lax.axis_index("slab") * band, band, 0
     )
@@ -418,15 +441,15 @@
         out_specs=(whole, whole),
         scratch_shapes=[
             room(2, cells, size_y, size_z),
-            room(chunks, node_count, total_x, rows, size_z),
-            room(chunks, total_x, rows, size_z),
-            room(total_x, node_count, rows, size_z),
-            room(total_x, node_count, rows, size_z),
-            room(chunks, SWEEPS + 1, total_x, rows, size_z),
+            room(chunks, node_count, total_x, rows, lanes),
+            room(chunks, total_x, rows, lanes),
+            room(total_x, node_count, rows, lanes),
+            room(total_x, node_count, rows, lanes),
+            room(chunks, SWEEPS + 1, total_x, rows, lanes),
             room(SWEEPS + 1, cells, size_y, size_z),
-            room(node_count, rows, size_z),
-            room(node_count, rows, size_z),
-            room(node_count, rows, size_z),
+            room(node_count, rows, lanes),
+            room(node_count, rows, lanes),
+            room(node_count, rows, lanes),
             room(8, 128),
             room(slab_count, 8, 128),
             room(node_count, 8, 128),

time: 125 us -> 119 us (0.952)
  Pallas kernels: 117 us -> 112 us
    pallas_call x1, Pallas kernels: 117 us -> 112 us  [on_device(): pl.pallas_call(functools.partial(sweeps_kernel, nodes, quad), out_shape=(...]
where the time goes in v3:
time: 119 us
  Pallas kernels  112 us (94%)
  local copies, waits for them, and re-layouts  3.66 us (3%)
  other arithmetic  2.58 us (2%)
    pallas_call x1, Pallas kernels, on_device(): pl.pallas_call(functools.partial(sweeps_kernel, nodes, quad), out_shape=(...  112 us
    unnamed x3, local copies, waits for them, and re-layouts  2.96 us

profile of v3, /device:TPU:0, one launch (start us, length us, event | category | flops | bytes accessed | tf_op | source)
XLA Modules:
  0.0 118.8 jit_solution(5500130200055909120)
XLA Ops:
  0.7 0.1 dynamic_slice.3
  0.8 0.7 broadcast_add_fusion.lam
  1.5 1.1 reduce-precision_convert_fusion
  2.6 0.7 pad_maximum_fusion.ymat_ref.zmat_ref
  3.3 111.9 %shard_map.41 = (f32[4,256,256]{2,1,0:T(8,128)}, f32[8,128]{1,0:T(8,128)}) custom-call(f32[4,256,256]{2,1,0:T(8,128)} %bitcast.3, f32[4,256,256]{2,1,0:T(8,128)} %first.1, f32[32,256]{1,0:T(8,128)} %broadcast_add_fusion.lam, bf16[2,256,256]{2,1,0:T(8,128)(2,1)} %pad_maximum_fusion.ymat_ref.zmat_ref, bf16[2,256,256]{2,1,0:T(8,128)(2,1)} %pad_maximum_fusion.ymat_ref.zmat_ref), custom_call_target="tpu_custom_call" | custom-call | tf_op jit(solution)/shard_map/pallas_call | solution.py:434
  115.2 0.0 copy-start
  115.3 0.7 copy-done
  115.9 0.6 slice_reduce_fusion
  116.5 2.3 %copy.5 = f32[1,4,256,256]{3,2,1,0:T(8,128)} copy(f32[1,4,256,256]{3,2,1,0:T(8,128)} %bitcast.2) | data formatting | bytes 2097152
  (1 shorter events, 0.0 us)
Async XLA Ops:
  115.2 0.7 copy-start

commit v4 on v3

--- a/solution.py
+++ b/solution.py
@@ -3,6 +3,7 @@
 
 import jax
 import jax.numpy as jnp
+import numpy as np
 from jax import lax
 from jax.experimental import pallas as pl
 from jax.experimental.pallas import tpu as pltpu
@@ -63,10 +64,9 @@
 
 
 def cas_table(length):
-    indices = lax.iota(jnp.int32, length)
-    products = indices[:, None] * indices[None, :] % length
-    phases = products.astype(jnp.float32) * (2.0 * math.pi / length)
-    return jnp.cos(phases) + jnp.sin(phases)
+    indices = np.arange(length)
+    phases = (indices[:, None] * indices[None, :] % length) * (2.0 * math.pi / length)
+    return (np.cos(phases) + np.sin(phases)).astype(np.float32)
 
 
 def eigen_line(length):
@@ -81,8 +81,9 @@
 
 
 def table_terms(table):
-    upper = lax.reduce_precision(table, 8, 7)
-    return jnp.stack([upper.astype(jnp.bfloat16), (table - upper).astype(jnp.bfloat16)])
+    upper = table.astype(jnp.bfloat16)
+    lower = (table - upper.astype(np.float32)).astype(jnp.bfloat16)
+    return jnp.asarray(np.stack([upper, lower]))
 
 
 def product(left, right):

time: 119 us -> 117 us (0.983)
  other arithmetic: 2.58 us -> 0.74 us
where the time goes in v4:
time: 117 us
  Pallas kernels  112 us (96%)
  local copies, waits for them, and re-layouts  3.66 us (3%)
    pallas_call x1, Pallas kernels, on_device(): pl.pallas_call(functools.partial(sweeps_kernel, nodes, quad), out_shape=(...  112 us
    unnamed x3, local copies, waits for them, and re-layouts  2.95 us

profile of v4, /device:TPU:0, one launch (start us, length us, event | category | flops | bytes accessed | tf_op | source)
XLA Modules:
  0.0 117.0 jit_solution(7695561002050414016)
XLA Ops:
  0.7 0.1 dynamic_slice.3
  0.8 0.7 broadcast_add_fusion.lam
  1.4 111.9 %shard_map.59 = (f32[4,256,256]{2,1,0:T(8,128)}, f32[8,128]{1,0:T(8,128)}) custom-call(f32[4,256,256]{2,1,0:T(8,128)} %bitcast.3, f32[4,256,256]{2,1,0:T(8,128)} %first.1, f32[32,256]{1,0:T(8,128)} %broadcast_add_fusion.lam, bf16[2,256,256]{2,1,0:T(8,128)(2,1)} %constant.18.clone.ymat_ref.zmat_ref, bf16[2,256,256]{2,1,0:T(8,128)(2,1)} %constant.18.clone.ymat_ref.zmat_ref), custom_call_target="tpu_custom_call" | custom-call | tf_op jit(solution)/shard_map/pallas_call | solution.py:435
  113.4 0.0 copy-start
  113.4 0.7 copy-done
  114.1 0.6 slice_reduce_fusion
  114.7 2.3 %copy.7 = f32[1,4,256,256]{3,2,1,0:T(8,128)} copy(f32[1,4,256,256]{3,2,1,0:T(8,128)} %bitcast.2) | data formatting | bytes 2097152
  (1 shorter events, 0.0 us)
Async XLA Ops:
  113.4 0.7 copy-start
